TPU v7x, 32 devices: a whole 2x2x4 slice. The times are simulated.
32 devices in a mesh: lat: 4 (over y, x), lon: 8 (over z, core).
Axes of the slice: x: 2, y: 2, z: 4, core: 2. Of those that a mesh axis runs over, the one named last changes fastest.
Arguments:
- activations: bfloat16 [4, 16, 720, 512], P(None, 'lat', 'lon'), may hold values from -48 to 48
- upstream: bfloat16 [4, 16, 720, 512], P(None, 'lat', 'lon'), may hold values from -6 to 6
- master: float32 [512, 9, 512], P(('lat', 'lon')), may hold values from -0.09375 to 0.09375
- moment_one: float32 [512, 9, 512], P(('lat', 'lon')), may hold values from -2.5 to 2.5
- moment_two: float32 [512, 9, 512], P(('lat', 'lon')), may hold values from 0.01 to 1
Outputs:
- input_grad: bfloat16 [4, 16, 720, 512], P(None, 'lat', 'lon')
- new_weights: bfloat16 [512, 9, 512], replicated
- new_master: float32 [512, 9, 512], P(('lat', 'lon'))
- new_moment_one: float32 [512, 9, 512], P(('lat', 'lon'))
- new_moment_two: float32 [512, 9, 512], P(('lat', 'lon'))
- clipped_grad: float32 [512, 9, 512], P(('lat', 'lon'))
All inputs are finite; a program needn't handle non-finite values.
Results may differ from a plain program's by a relative error of at most 0.0049.
Values may be sent and summed in bfloat16 or wider, within the bound.
A program may use at most 128 MiB of HBM per device.

v0:
```python
import math

import jax
import jax.numpy as jnp
from jax import lax
from jax.sharding import PartitionSpec as P

CIN = 512
COUT = 512
TAPS = 9


learn_rate = 0.01
beta_one = 0.9
beta_two = 0.999
adam_eps = 1e-08
decay_rate = 0.1
step_count = 10.0
norm_eps = 1e-06


def padded(block, sides, width):
    for axis, dim in sides:
        count = lax.axis_size(axis)
        forward = [(i, i + 1) for i in range(count - 1)]
        forward.append((count - 1, 0))
        backward = [(target, source) for source, target in forward]
        low = lax.ppermute(
            lax.slice_in_dim(block, block.shape[dim] - width, None, axis=dim), axis, forward
        )
        high = lax.ppermute(lax.slice_in_dim(block, 0, width, axis=dim), axis, backward)
        block = jnp.concatenate([low, block, high], axis=dim)
    return block


def mask_poles(wide_field):
    lat_index = lax.axis_index("lat")
    lat_count = lax.axis_size("lat")
    total_rows = wide_field.shape[1]
    row_ids = lax.broadcasted_iota(jnp.int32, (1, total_rows, 1, 1), 1)
    upper = jnp.logical_and(row_ids == 0, lat_index == 0)
    lower = jnp.logical_and(row_ids == total_rows - 1, lat_index == lat_count - 1)
    return jnp.where(jnp.logical_or(upper, lower), jnp.zeros((), wide_field.dtype), wide_field)


def pull_product(grad_wide, lat_rows, lon_cols):
    batch_rows = grad_wide.shape[0]
    out_width = grad_wide.shape[3]
    windows = []
    for tap_index in range(9):
        row_off, col_off = divmod(tap_index, 3)
        windows.append(
            grad_wide[
                :, 2 - row_off : 2 - row_off + lat_rows, 2 - col_off : 2 - col_off + lon_cols, :
            ].reshape(-1, out_width)
        )

    def pull_compute(shard_piece, first_row):
        piece_width = shard_piece.shape[0]
        summed = jnp.zeros((batch_rows * lat_rows * lon_cols, piece_width), jnp.float32)
        for tap_index in range(9):
            summed = summed + lax.dot_general(
                windows[tap_index],
                shard_piece[:, tap_index, :],
                (((1,), (1,)), ((), ())),
                preferred_element_type=jnp.float32,
            )
        return summed.reshape(batch_rows, lat_rows, lon_cols, piece_width)

    return pull_compute


def input_taps(act_wide, grad_flat, lat_rows, lon_cols):

    def input_compute(first_row, row_count):
        tap_parts = []
        for tap_index in range(9):
            row_off, col_off = divmod(tap_index, 3)
            tap_slab = act_wide[
                :, row_off : row_off + lat_rows, col_off : col_off + lon_cols, :
            ].reshape(-1, row_count)
            tap_parts.append(
                lax.dot_general(
                    tap_slab,
                    grad_flat,
                    (((0,), (0,)), ((), ())),
                    preferred_element_type=jnp.float32,
                )
            )
        return jnp.stack(tap_parts, axis=1)

    return input_compute


def per_device(activations, upstream, master, moment_one, moment_two):
    lat_rows = activations.shape[1]
    lon_cols = activations.shape[2]
    grad_flat = upstream.reshape(-1, upstream.shape[3])
    act_wide = mask_poles(padded(activations, (("lat", 1), ("lon", 2)), 1))
    grad_wide = mask_poles(padded(upstream, (("lat", 1), ("lon", 2)), 1))
    producer = pull_product(grad_wide, lat_rows, lon_cols)
    term_maker = input_taps(act_wide, grad_flat, lat_rows, lon_cols)
    old_weights = master.astype(jnp.bfloat16)
    old_block = lax.all_gather(old_weights, "lon", axis=0, tiled=True)
    data_sum = producer(lax.all_gather(old_block, "lat", axis=0, tiled=True), jnp.int32(0))
    input_grad = data_sum.astype(jnp.bfloat16)
    shard_rows = master.shape[0]
    lat_block = lax.psum_scatter(
        term_maker(jnp.int32(0), lax.axis_size("lat") * (shard_rows * lax.axis_size("lon"))),
        "lat",
        scatter_dimension=0,
        tiled=True,
    )
    grad_shard = lax.psum_scatter(lat_block, "lon", scatter_dimension=0, tiled=True)
    max_norm = math.sqrt(float(CIN * TAPS * COUT))
    square_sum = lax.psum(jnp.sum(grad_shard * grad_shard), ("lat", "lon"))
    clip_factor = jnp.minimum(1.0, max_norm / (jnp.sqrt(square_sum) + norm_eps))
    grad_scaled = clip_factor * grad_shard
    new_one = beta_one * moment_one + (1.0 - beta_one) * grad_scaled
    new_two = beta_two * moment_two + (1.0 - beta_two) * grad_scaled * grad_scaled
    first_hat = new_one / (1.0 - beta_one**step_count)
    second_hat = new_two / (1.0 - beta_two**step_count)
    new_master = master - learn_rate * (
        first_hat / (jnp.sqrt(second_hat) + adam_eps) + decay_rate * master
    )
    new_half = new_master.astype(jnp.bfloat16)
    lon_block = lax.all_gather(new_half, "lon", axis=0, tiled=True)
    new_weights = lax.all_gather(lon_block, "lat", axis=0, tiled=True)
    return (input_grad, new_weights, new_master, new_one, new_two, grad_scaled)


def solution(mesh):
    in_specs = (
        P(None, "lat", "lon", None),
        P(None, "lat", "lon", None),
        P(("lat", "lon"), None, None),
        P(("lat", "lon"), None, None),
        P(("lat", "lon"), None, None),
    )
    out_specs = (
        P(None, "lat", "lon", None),
        P(),
        P(("lat", "lon"), None, None),
        P(("lat", "lon"), None, None),
        P(("lat", "lon"), None, None),
        P(("lat", "lon"), None, None),
    )
    return jax.shard_map(
        per_device, mesh=mesh, in_specs=in_specs, out_specs=out_specs, check_vma=False
    )
```

profile of v0, /device:TPU:0, one launch (start us, length us, event | category | flops | bytes accessed | tf_op | source)
XLA Modules:
  0.0 431.5 jit_solution(1120258594187733168)
XLA Ops:
  7.2 3.2 fusion.90
  11.2 3.0 collective-permute-start
  20.8 4.6 %collective-permute-done = bf16[4,1,90,512]{3,2,1,0:T(8,128)(2,1)} collective-permute-done((bf16[4,1,90,512]{3,2,1,0:T(8,128)(2,1)}, bf16[4,1,90,512]{3,2,1,0:T(8,128)(2,1)}, u32[]{:S(2)}, u32[]{:S(2)}) %collective-permute-start) | collective-permute-done | bytes 368672 | tf_op jit(solution)/shard_map/ppermute | solution.py:28
  26.8 7.6 %collective-permute-done.1 = bf16[4,1,90,512]{3,2,1,0:T(8,128)(2,1)} collective-permute-done((bf16[4,1,90,512]{3,2,1,0:T(8,128)(2,1)}, bf16[4,1,90,512]{3,2,1,0:T(8,128)(2,1)}, u32[]{:S(2)}, u32[]{:S(2)}) %collective-permute-start.1) | collective-permute-done | bytes 368672 | tf_op jit(solution)/shard_map/ppermute | solution.py:31
  35.6 3.5 collective-permute-start.3
  39.1 3.2 collective-permute-done.4
  43.7 6.5 %collective-permute-done.5 = bf16[4,1,90,512]{3,2,1,0:T(8,128)(2,1)} collective-permute-done((bf16[4,1,90,512]{3,2,1,0:T(8,128)(2,1)S(1)}, bf16[4,1,90,512]{3,2,1,0:T(8,128)(2,1)}, u32[]{:S(2)}, u32[]{:S(2)}) %collective-permute-start.5) | collective-permute-done | bytes 368672 | tf_op jit(solution)/shard_map/ppermute | solution.py:31
  51.3 3.5 collective-permute-start.7
  56.7 2.7 maximum_select_fusion.1
  61.3 2.0 fusion.28
  63.3 2.0 fusion.34
  67.4 2.1 fusion.46
  69.4 2.0 fusion.52
  73.4 2.1 fusion.64
  75.5 2.0 fusion.70
  77.7 95.2 %reduce-scatter.3.cloned.1.call-done = f32[128,9,512]{2,0,1:T(8,128)} async-done(((f32[512,9,512]{2,0,1:T(8,128)}), f32[128,9,512]{2,0,1:T(8,128)}) %reduce-scatter.3.cloned.1.call-update) | async-done | bytes 2359312 | tf_op jit(solution)/shard_map/reduce_scatter | solution.py:108
  173.0 39.4 %reduce-scatter.5.cloned.1.call-done = f32[16,9,512]{2,0,1:T(8,128)} async-done(((f32[128,9,512]{2,0,1:T(8,128)}), f32[16,9,512]{2,0,1:T(8,128)}) %reduce-scatter.5.cloned.1.call-update) | async-done | bytes 294928 | tf_op jit(solution)/shard_map/reduce_scatter | solution.py:114
  214.0 37.9 %psum.7 = f32[]{:T(128)} all-reduce(f32[]{:T(128)} %multiply_reduce_fusion), channel_id=1, replica_groups=mesh['lat'=4,'lon'=8] {'lat','lon'}, use_global_device_ids=true, to_apply=%region_3.4 | all-reduce | flops 1 | bytes 8 | tf_op jit(solution)/shard_map/psum | solution.py:116
  252.6 2.2 fusion.84
  255.4 23.0 %all-gather.5.cloned.1.call-done = bf16[128,9,512]{2,0,1:T(8,128)(2,1)} async-done(((bf16[16,9,512]{2,0,1:T(8,128)(2,1)}), bf16[128,9,512]{2,0,1:T(8,128)(2,1)}) %all-gather.5.cloned.1.call-update) | async-done | bytes 1179664 | tf_op jit(solution)/shard_map/all_gather | solution.py:104
  278.7 24.2 %all-gather.9.cloned.1.call-done = bf16[128,9,512]{2,0,1:T(8,128)(2,1)} async-done(((bf16[16,9,512]{2,0,1:T(8,128)(2,1)}), bf16[128,9,512]{2,0,1:T(8,128)(2,1)}) %all-gather.9.cloned.1.call-update) | async-done | bytes 1179664 | tf_op jit(solution)/shard_map/all_gather | solution.py:127
  302.9 6.2 %fusion.87 = (bf16[4,4,90,512]{3,2,1,0:T(8,128)(2,1)}, bf16[4,4,90,512]{3,2,1,0:T(8,128)(2,1)}, bf16[4,4,90,512]{3,2,1,0:T(8,128)(2,1)}, bf16[4,4,90,512]{3,2,1,...) fusion(bf16[4,6,92,512]{3,2,1,0:T(8,128)(2,1)S(1)} %get-tuple-e, ...), kind=kLoop, calls=%fused_computation.81 | loop fusion | bytes 26542080 | tf_op jit(solution)/shard_map/slice | solution.py:53
  310.9 2.7 reshape.67
  314.9 2.6 reshape.69
  317.5 2.4 reshape.70
  321.2 2.6 reshape.72
  323.8 2.5 reshape.73
  327.6 33.6 %all-gather.7.cloned.1.call-done = bf16[512,9,512]{2,0,1:T(8,128)(2,1)} async-done(((bf16[128,9,512]{2,0,1:T(8,128)(2,1)}), bf16[512,9,512]{2,0,1:T(8,128)(2,1)}) %all-gather.7.cloned.1.call-update) | async-done | bytes 4718608 | tf_op jit(solution)/shard_map/all_gather | solution.py:105
  361.2 2.2 fusion.73
  375.2 2.3 copy.42
  377.4 42.5 %all-gather.11.cloned.1.call-done = bf16[512,9,512]{2,0,1:T(8,128)(2,1)} async-done(((bf16[128,9,512]{2,0,1:T(8,128)(2,1)}), bf16[512,9,512]{2,0,1:T(8,128)(2,1)}) %all-gather.11.cloned.1.call-update) | async-done | bytes 4718608 | tf_op jit(solution)/shard_map/all_gather | solution.py:128
  419.9 4.8 %copy.89 = bf16[512,9,512]{2,0,1:T(8,128)(2,1)} copy(bf16[512,9,512]{2,0,1:T(8,128)(2,1)} %all-gather.11.cloned.1.call-done) | data formatting | bytes 9437184
  (88 shorter events, 40.3 us)
Async XLA Ops:
  7.2 8.8 %copy-start.3 = (bf16[4,4,90,512]{3,1,2,0:T(4,128)(2,1)S(1)}, bf16[4,4,90,512]{3,1,2,0:T(4,128)(2,1)}, u32[]{:S(2)}) copy-start(bf16[4,4,90,512]{3,1,2,0:T(4,128)(2,1)} %param.5) | copy-start | bytes 4423684
  7.2 165.7 %reduce-scatter.3.cloned.1.call-start = ((), (), s32[]{:S(2)}) async-start(), calls=%async_computation.4 | async-start | bytes 11796480 | tf_op jit(solution)/shard_map/reduce_scatter | solution.py:108
  11.2 14.2 %collective-permute-start = (bf16[4,1,90,512]{3,2,1,0:T(8,128)(2,1)}, bf16[4,1,90,512]{3,2,1,0:T(8,128)(2,1)}, u32[]{:S(2)}, u32[]{:S(2)}) collective-permute-start(bf16[4,1,90,512]{3,2,1,0:T(8,128)(2,1)} %copy.72), channel_id=1, source_target_pairs={{0,8},{8,16},{16,24},{24,0},{1,9},{9,17},{17,25},{25,1},{2,10},{10... | collective-permute-start | bytes 1105928 | tf_op jit(solution)/shard_map/ppermute | solution.py:28
  15.0 11.5 %copy-start.4 = (bf16[4,4,90,512]{3,1,2,0:T(4,128)(2,1)S(1)}, bf16[4,4,90,512]{3,1,2,0:T(4,128)(2,1)}, u32[]{:S(2)}) copy-start(bf16[4,4,90,512]{3,1,2,0:T(4,128)(2,1)} %param.6) | copy-start | bytes 4423684
  15.0 19.4 %collective-permute-start.1 = (bf16[4,1,90,512]{3,2,1,0:T(8,128)(2,1)}, bf16[4,1,90,512]{3,2,1,0:T(8,128)(2,1)}, u32[]{:S(2)}, u32[]{:S(2)}) collective-permute-start(bf16[4,1,90,512]{3,2,1,0:T(8,128)(2,1)} %copy.73), channel_id=1, source_target_pairs={{8,0},{16,8},{24,16},{0,24},{9,1},{17,9},{25,17},{1,25},{10,2},{18... | collective-permute-start | bytes 1105928 | tf_op jit(solution)/shard_map/ppermute | solution.py:31
  17.8 24.5 %collective-permute-start.4 = (bf16[4,1,90,512]{3,2,1,0:T(8,128)(2,1)}, bf16[4,1,90,512]{3,2,1,0:T(8,128)(2,1)}, u32[]{:S(2)}, u32[]{:S(2)}) collective-permute-start(bf16[4,1,90,512]{3,2,1,0:T(8,128)(2,1)} %copy.74), channel_id=1, source_target_pairs={{0,8},{8,16},{16,24},{24,0},{1,9},{9,17},{17,25},{25,1},{2,10},{10... | collective-permute-start | bytes 1105928 | tf_op jit(solution)/shard_map/ppermute | solution.py:28
  18.9 31.2 %collective-permute-start.5 = (bf16[4,1,90,512]{3,2,1,0:T(8,128)(2,1)S(1)}, bf16[4,1,90,512]{3,2,1,0:T(8,128)(2,1)}, u32[]{:S(2)}, u32[]{:S(2)}) collective-permute-start(bf16[4,1,90,512]{3,2,1,0:T(8,128)(2,1)S(1)} %copy.75), channel_id=1, source_target_pairs={{8,0},{16,8},{24,16},{0,24},{9,1},{17,9},{25,17},{1,25},{10,2},{18... | collective-permute-start | bytes 1105928 | tf_op jit(solution)/shard_map/ppermute | solution.py:31
  35.5 19.3 %collective-permute-start.2 = (bf16[4,6,1,512]{3,2,1,0:T(2,128)(2,1)S(1)}, bf16[4,6,1,512]{3,2,1,0:T(2,128)(2,1)S(1)}, u32[]{:S(2)}, u32[]{:S(2)}) collective-permute-start(bf16[4,6,1,512]{3,2,1,0:T(2,128)(2,1)S(1)} %get-tuple-element.34), channel_id=1, source_target_pairs={{0,1},{1,2},{2,3},{3,4},{4,5},{5,6},{6,7},{7,0},{8,9},{9,10},{10,1... | collective-permute-start | bytes 73736 | tf_op jit(solution)/shard_map/ppermute | solution.py:28
  35.6 19.3 %collective-permute-start.3 = (bf16[4,6,1,512]{3,2,1,0:T(2,128)(2,1)S(1)}, bf16[4,6,1,512]{3,2,1,0:T(2,128)(2,1)S(1)}, u32[]{:S(2)}, u32[]{:S(2)}) collective-permute-start(bf16[4,6,1,512]{3,2,1,0:T(2,128)(2,1)S(1)} %get-tuple-element.35), channel_id=1, source_target_pairs={{1,0},{2,1},{3,2},{4,3},{5,4},{6,5},{7,6},{0,7},{9,8},{10,9},{11,1... | collective-permute-start | bytes 73736 | tf_op jit(solution)/shard_map/ppermute | solution.py:31
  51.2 5.4 %collective-permute-start.6 = (bf16[4,6,1,512]{3,2,1,0:T(2,128)(2,1)S(1)}, bf16[4,6,1,512]{3,2,1,0:T(2,128)(2,1)S(1)}, u32[]{:S(2)}, u32[]{:S(2)}) collective-permute-start(bf16[4,6,1,512]{3,2,1,0:T(2,128)(2,1)S(1)} %get-tuple-element.23), channel_id=1, source_target_pairs={{0,1},{1,2},{2,3},{3,4},{4,5},{5,6},{6,7},{7,0},{8,9},{9,10},{10,1... | collective-permute-start | bytes 73736 | tf_op jit(solution)/shard_map/ppermute | solution.py:28
  51.3 5.3 %collective-permute-start.7 = (bf16[4,6,1,512]{3,2,1,0:T(2,128)(2,1)S(1)}, bf16[4,6,1,512]{3,2,1,0:T(2,128)(2,1)S(1)}, u32[]{:S(2)}, u32[]{:S(2)}) collective-permute-start(bf16[4,6,1,512]{3,2,1,0:T(2,128)(2,1)S(1)} %get-tuple-element.24), channel_id=1, source_target_pairs={{1,0},{2,1},{3,2},{4,3},{5,4},{6,5},{7,6},{0,7},{9,8},{10,9},{11,1... | collective-permute-start | bytes 73736 | tf_op jit(solution)/shard_map/ppermute | solution.py:31
  54.8 4.5 %copy-start.5 = (bf16[4,4,90,512]{3,1,2,0:T(4,128)(2,1)S(1)}, bf16[4,4,90,512]{3,1,2,0:T(4,128)(2,1)}, u32[]{:S(2)}) copy-start(bf16[4,4,90,512]{3,1,2,0:T(4,128)(2,1)} %param.6) | copy-start | bytes 4423684
  77.6 175.0 %copy-start.15 = (f32[16,9,512]{2,0,1:T(8,128)S(1)}, f32[16,9,512]{2,0,1:T(8,128)}, u32[]{:S(2)}) copy-start(f32[16,9,512]{2,0,1:T(8,128)} %param.7) | copy-start | bytes 884740
  77.6 175.0 %copy-start.16 = (f32[16,9,512]{2,0,1:T(8,128)S(1)}, f32[16,9,512]{2,0,1:T(8,128)}, u32[]{:S(2)}) copy-start(f32[16,9,512]{2,0,1:T(8,128)} %param.8) | copy-start | bytes 884740
  77.6 175.0 %copy-start.17 = (f32[16,9,512]{2,0,1:T(8,128)S(1)}, f32[16,9,512]{2,0,1:T(8,128)}, u32[]{:S(2)}) copy-start(f32[16,9,512]{2,0,1:T(8,128)} %param.9) | copy-start | bytes 884740
  77.6 134.7 %reduce-scatter.5.cloned.1.call-start = ((), (), s32[]{:S(2)}) async-start(), calls=%async_computation.5 | async-start | bytes 2654208 | tf_op jit(solution)/shard_map/reduce_scatter | solution.py:114
  172.9 105.5 %all-gather.5.cloned.1.call-start = ((), (), s32[]{:S(2)}) async-start(), calls=%async_computation.2 | async-start | bytes 1327104 | tf_op jit(solution)/shard_map/all_gather | solution.py:104
  254.8 48.1 %all-gather.9.cloned.1.call-start = ((), (), s32[]{:S(2)}) async-start(), calls=%async_computation.6 | async-start | bytes 1327104 | tf_op jit(solution)/shard_map/all_gather | solution.py:127
  255.4 105.8 %all-gather.7.cloned.1.call-start = ((), (), s32[]{:S(2)}) async-start(), calls=%async_computation.3 | async-start | bytes 5898240 | tf_op jit(solution)/shard_map/all_gather | solution.py:105
  278.4 141.5 %all-gather.11.cloned.1.call-start = ((), (), s32[]{:S(2)}) async-start(), calls=%async_computation.7 | async-start | bytes 5898240 | tf_op jit(solution)/shard_map/all_gather | solution.py:128
  309.1 4.4 %copy-start.2 = (bf16[4,4,90,512]{3,2,1,0:T(8,128)(2,1)S(1)}, bf16[4,4,90,512]{3,2,1,0:T(8,128)(2,1)}, u32[]{:S(2)}) copy-start(bf16[4,4,90,512]{3,2,1,0:T(8,128)(2,1)} %get-tuple-element.31) | copy-start | bytes 4423684
  314.9 5.0 %copy-start.1 = (bf16[4,4,90,512]{3,2,1,0:T(8,128)(2,1)S(1)}, bf16[4,4,90,512]{3,2,1,0:T(8,128)(2,1)}, u32[]{:S(2)}) copy-start(bf16[4,4,90,512]{3,2,1,0:T(8,128)(2,1)} %get-tuple-element.28) | copy-start | bytes 4423684
  321.2 5.1 %copy-start = (bf16[4,4,90,512]{3,2,1,0:T(8,128)(2,1)S(1)}, bf16[4,4,90,512]{3,2,1,0:T(8,128)(2,1)}, u32[]{:S(2)}) copy-start(bf16[4,4,90,512]{3,2,1,0:T(8,128)(2,1)} %get-tuple-element.25) | copy-start | bytes 4423684
  327.6 35.8 %copy-start.13 = (bf16[1440,512]{1,0:T(8,128)(2,1)S(1)}, bf16[1440,512]{1,0:T(8,128)(2,1)}, u32[]{:S(2)}) copy-start(bf16[1440,512]{1,0:T(8,128)(2,1)} %reshape.67) | copy-start | bytes 4423684
  361.2 2.5 copy-start.14
  363.7 1.4 copy-start.12
  365.1 1.4 copy-start.11
  366.5 1.4 copy-start.10
  367.8 1.4 copy-start.9
  369.2 1.6 copy-start.8
  370.8 1.5 copy-start.7
  372.3 1.5 copy-start.6
Sparse Core Ops, SparseCore 0:
  77.7 95.1 reduce-scatter.2
  175.2 37.0 reduce-scatter.4
  254.9 23.4 all-gather.4
  280.4 22.4 all-gather.8
  304.6 56.5 all-gather.6
  362.9 56.9 all-gather.10
where the time goes:
time: 432 us
  waiting for transfers between devices  282 us (65%)
  local copies, waits for them, and re-layouts  47.3 us (11%)
  blocking collectives  37.9 us (9%)
  matrix products  28.2 us (7%)
  between operations  15.1 us (3%)
  starting transfers between devices  14.5 us (3%)
  other arithmetic  6.48 us (2%)
    reduce_scatter x1, waiting for transfers between devices, per_device(): lax.psum_scatter(term_maker(jnp.int32(0), lax.axis_size('lat') * (shard_r...  95.2 us
    all_gather x1, waiting for transfers between devices, per_device(): new_weights = lax.all_gather(lon_block, 'lat', axis=0, tiled=True)  42.5 us
    reduce_scatter x1, waiting for transfers between devices, per_device(): lax.psum_scatter(lat_block, 'lon', scatter_dimension=0, tiled=True)  39.4 us
    psum x1, blocking collectives, per_device(): square_sum = lax.psum(jnp.sum(grad_shard * grad_shard), ('lat', 'lon'))  37.9 us
    all_gather x1, waiting for transfers between devices, per_device(): lax.all_gather(old_block, 'lat', axis=0, tiled=True)  33.6 us
    all_gather x1, waiting for transfers between devices, per_device(): lon_block = lax.all_gather(new_half, 'lon', axis=0, tiled=True)  24.2 us
    all_gather x1, waiting for transfers between devices, per_device(): old_block = lax.all_gather(old_weights, 'lon', axis=0, tiled=True)  23 us
    reshape x9, local copies, waits for them, and re-layouts, pull_product(): windows.append(grad_wide[:, 2 - row_off:2 - row_off + lat_rows, 2 - col_o...  18.5 us
  transfers between devices with their start and end apart: 14, of which 11 were waited for; matrix products, arithmetic and copies ran while one was open for 10% of the time, Pallas kernels for 0%

commit v1 on v0

v1 whole, which is shorter than its diff:
```python
import functools
import math

import jax
import jax.numpy as jnp
from jax import lax
from jax.experimental import pallas as pl
from jax.experimental.pallas import tpu as pltpu
from jax.sharding import PartitionSpec as P

MESH = pl.DeviceIdType.MESH

CIN = 512
COUT = 512
TAPS = 9


learn_rate = 0.01
beta_one = 0.9
beta_two = 0.999
adam_eps = 1e-08
decay_rate = 0.1
step_count = 10.0
norm_eps = 1e-06


def halo_kernel(n_lat, n_lon, *refs):
    sources, landings, (send_sem, recv_sem) = refs[:8], refs[8:16], refs[16:]
    lat, lon = lax.axis_index("lat"), lax.axis_index("lon")
    steps = ((-1, 0), (1, 0), (0, -1), (0, 1), (-1, -1), (-1, 1), (1, -1), (1, 1))
    targets = [
        (lax.rem(lat + dy + n_lat, n_lat), lax.rem(lon + dx + n_lon, n_lon)) for dy, dx in steps
    ]
    barrier = pltpu.get_barrier_semaphore()
    for target in targets:
        pl.semaphore_signal(barrier, inc=1, device_id=target, device_id_type=MESH)
    pl.semaphore_wait(barrier, len(targets))
    copies = []
    for index, target in enumerate(targets):
        copy = pltpu.make_async_remote_copy(
            src_ref=sources[index], dst_ref=landings[index], send_sem=send_sem.at[index],
            recv_sem=recv_sem.at[index], device_id=target, device_id_type=MESH,
        )
        copy.start()
        copies.append(copy)
    for copy in copies:
        copy.wait()


def widened(fields):
    both = jnp.stack(fields)
    top, bottom = both[:, :, 0], both[:, :, -1]
    pieces = (
        top, bottom, both[:, :, :, 0], both[:, :, :, -1],
        top[:, :, 0], top[:, :, -1], bottom[:, :, 0], bottom[:, :, -1],
    )
    landed = pl.pallas_call(
        functools.partial(halo_kernel, lax.axis_size("lat"), lax.axis_size("lon")),
        out_shape=tuple(jax.ShapeDtypeStruct(p.shape, p.dtype) for p in pieces),
        in_specs=[pl.BlockSpec(memory_space=pltpu.VMEM)] * 8,
        out_specs=(pl.BlockSpec(memory_space=pltpu.VMEM),) * 8,
        scratch_shapes=[pltpu.SemaphoreType.DMA((8,)), pltpu.SemaphoreType.DMA((8,))],
        compiler_params=pltpu.CompilerParams(
            collective_id=1, has_side_effects=True, vmem_limit_bytes=24 * 1024 * 1024
        ),
        name="halo",
    )(*pieces)
    below, above, east, west, below_east, below_west, above_east, above_west = landed

    def row(start, middle, end):
        return jnp.concatenate([start[:, None, None], middle[:, None], end[:, None, None]], axis=2)

    wide = []
    for index, field in enumerate(fields):
        middle = jnp.concatenate(
            [west[index][:, :, None], field, east[index][:, :, None]], axis=2
        )
        first = row(above_west[index], above[index], above_east[index])
        last = row(below_west[index], below[index], below_east[index])
        wide.append(mask_poles(jnp.concatenate([first, middle, last], axis=1)))
    return wide


def mask_poles(wide_field):
    lat_index = lax.axis_index("lat")
    lat_count = lax.axis_size("lat")
    total_rows = wide_field.shape[1]
    row_ids = lax.broadcasted_iota(jnp.int32, (1, total_rows, 1, 1), 1)
    upper = jnp.logical_and(row_ids == 0, lat_index == 0)
    lower = jnp.logical_and(row_ids == total_rows - 1, lat_index == lat_count - 1)
    return jnp.where(jnp.logical_or(upper, lower), jnp.zeros((), wide_field.dtype), wide_field)


def input_taps(act_wide, grad_flat, lat_rows, lon_cols):

    def input_compute(first_row, row_count):
        tap_parts = []
        for tap_index in range(9):
            row_off, col_off = divmod(tap_index, 3)
            tap_slab = act_wide[
                :, row_off : row_off + lat_rows, col_off : col_off + lon_cols, :
            ].reshape(-1, row_count)
            tap_parts.append(
                lax.dot_general(
                    tap_slab,
                    grad_flat,
                    (((0,), (0,)), ((), ())),
                    preferred_element_type=jnp.float32,
                )
            )
        return jnp.stack(tap_parts, axis=1)

    return input_compute


def reduce_update_gather(
    n_lat, n_q, max_norm, part, master, one, two,
    gathered, new_master, new_one, new_two, clipped,
    core_in, sums, right_in, left_in, lat_out, lat_in, norm_out, norm_in,
    send_sem, recv_sem,
):
    lat = lax.axis_index("lat")
    lon = lax.axis_index("lon")
    core = lax.rem(lon, 2)
    q = lon // 2
    hops = n_q // 2
    half = n_lat // 2
    counter = [0]
    pending = []

    def at(lat_id, q_id, core_id):
        return (lat_id, q_id * 2 + core_id)

    partner = at(lat, q, 1 - core)
    right_q = lax.rem(q + 1, n_q)
    left_q = lax.rem(q + n_q - 1, n_q)
    right, left = at(lat, right_q, core), at(lat, left_q, core)
    q_peers = [at(lat, lax.rem(q + d, n_q), core) for d in range(1, n_q)]
    lat_peers = [at(lax.rem(lat + d, n_lat), q, core) for d in range(1, n_lat)]

    def send(src, dst, target):
        index = counter[0]
        counter[0] += 1
        copy = pltpu.make_async_remote_copy(
            src_ref=src, dst_ref=dst, send_sem=send_sem.at[index],
            recv_sem=recv_sem.at[index], device_id=target, device_id_type=MESH,
        )
        copy.start()
        pending.append(copy)
        return copy

    def wrap(index, size):
        return lax.rem(index + size, size)

    barrier = pltpu.get_barrier_semaphore()
    greeted = [partner] + q_peers + lat_peers
    for device in greeted:
        pl.semaphore_signal(barrier, inc=1, device_id=device, device_id_type=MESH)
    pl.semaphore_wait(barrier, len(greeted))

    order = []
    for step in range(hops):
        for block in (hops - step, -hops + step):
            if block % n_q not in order:
                order.append(block % n_q)
    order.append(0)
    core_copies = []
    for offset in order:
        block = lax.rem(q + offset, n_q)
        core_copies.append(
            send(part.at[:, :, block, 1 - core], core_in.at[:, :, block], partner)
        )
    arrived = {}

    def core_sum(offset):
        if offset in arrived:
            return
        arrived[offset] = True
        core_copies[order.index(offset)].wait_recv()
        block = lax.rem(q + offset, n_q)

        @pl.loop(0, n_lat)
        def _(row):
            sums[block, row] = (
                part[:, row, block, core] + core_in[:, row, block]
            ).astype(jnp.bfloat16)

    def add_into(block, low, high, source):
        @pl.loop(low, high)
        def _(row):
            sums[block, row] = (
                sums[block, row].astype(jnp.float32) + source[row].astype(jnp.float32)
            ).astype(jnp.bfloat16)

    ring = []
    for step in range(hops):
        right_off = (hops - step) % n_q
        left_off = (step - hops) % n_q
        core_sum(right_off)
        core_sum(left_off)
        right_block = lax.rem(q + right_off, n_q)
        left_block = lax.rem(q + left_off, n_q)
        if step == 0:
            ring.append((
                send(sums.at[right_block, pl.ds(0, half)], right_in.at[0, pl.ds(0, half)], right),
                send(sums.at[left_block, pl.ds(half, n_lat - half)],
                     left_in.at[0, pl.ds(half, n_lat - half)], left),
            ))
        else:
            from_left, from_right = ring[-1]
            bounds = (0, half, half, n_lat) if step == 1 else (0, n_lat, 0, n_lat)
            from_left.wait_recv()
            add_into(right_block, bounds[0], bounds[1], right_in.at[step - 1])
            going_right = send(sums.at[right_block], right_in.at[step], right)
            from_right.wait_recv()
            add_into(left_block, bounds[2], bounds[3], left_in.at[step - 1])
            ring.append((going_right, send(sums.at[left_block], left_in.at[step], left)))
    core_sum(0)
    for copy in ring[-1]:
        copy.wait_recv()

    def q_total(row):
        total = part[:, row, q, core] + core_in[:, row, q]
        if hops > 1:
            return (
                total + right_in[hops - 1, row].astype(jnp.float32)
                + left_in[hops - 1, row].astype(jnp.float32)
            )
        return total + jnp.where(
            row < half, right_in[0, row].astype(jnp.float32), left_in[0, row].astype(jnp.float32)
        )

    lat_copies = []
    for step in range(1, n_lat):
        target = lax.rem(lat + step, n_lat)
        lat_out[step - 1] = q_total(target).astype(jnp.bfloat16)
        lat_copies.append(send(lat_out.at[step - 1], lat_in.at[step - 1], lat_peers[step - 1]))
    grad = q_total(lat)
    for step, copy in enumerate(lat_copies):
        copy.wait_recv()
        grad = grad + lat_in[step].astype(jnp.float32)
    clipped[...] = grad

    square = jnp.sum(grad * grad)
    slot = 0
    for stage, peers in enumerate(([partner], q_peers, lat_peers)):
        norm_out[stage] = jnp.full(norm_out.shape[1:], square, jnp.float32)
        copies = []
        for target in peers:
            copies.append(send(norm_out.at[stage], norm_in.at[slot], target))
            slot += 1
        tile = norm_out[stage]
        for index, copy in enumerate(copies):
            copy.wait_recv()
            tile = tile + norm_in[slot - len(peers) + index]
        square = jnp.max(tile)
    square = jnp.full((1, 1), square, jnp.float32)
    clip_factor = jnp.minimum(1.0, max_norm / (jnp.sqrt(square) + norm_eps))

    @pl.loop(0, clipped.shape[0])
    def _(tap):
        scaled = clip_factor * clipped[tap]
        clipped[tap] = scaled
        first = beta_one * one[tap] + (1.0 - beta_one) * scaled
        second = beta_two * two[tap] + (1.0 - beta_two) * scaled * scaled
        new_one[tap] = first
        new_two[tap] = second
        first_hat = first / (1.0 - beta_one**step_count)
        second_hat = second / (1.0 - beta_two**step_count)
        updated = master[tap] - learn_rate * (
            first_hat / (jnp.sqrt(second_hat) + adam_eps) + decay_rate * master[tap]
        )
        new_master[tap] = updated
        gathered[core, q, lat, tap] = updated.astype(jnp.bfloat16)

    copies = [
        send(gathered.at[core, q, lat], gathered.at[core, q, lat], peer) for peer in lat_peers
    ]
    for copy in copies:
        copy.wait_recv()
    core_in_copies = []

    def to_partner(block, low, count):
        piece = gathered.at[core, block, pl.ds(low, count)]
        core_in_copies.append(send(piece, piece, partner))

    from_left = from_right = None
    for step in range(hops):
        last = step == hops - 1
        right_block = wrap(q - step, n_q)
        left_block = lax.rem(q + step, n_q)
        if from_left is not None:
            from_left.wait_recv()
        piece = gathered.at[core, right_block, pl.ds(0, half if last else n_lat)]
        going_right = send(piece, piece, right)
        if from_right is not None:
            from_right.wait_recv()
        low = half if last else 0
        piece = gathered.at[core, left_block, pl.ds(low, n_lat - low)]
        going_left = send(piece, piece, left)
        to_partner(right_block, 0, n_lat)
        if step > 0:
            to_partner(left_block, 0, n_lat)
        from_left, from_right = going_right, going_left
    far = lax.rem(q + hops, n_q)
    from_left.wait_recv()
    to_partner(far, 0, half)
    from_right.wait_recv()
    to_partner(far, half, n_lat - half)
    for copy in core_in_copies:
        copy.wait_recv()
    for copy in pending:
        copy.wait_send()


def fused_update(partial, master, one, two):
    n_lat, n_q = lax.axis_size("lat"), lax.axis_size("lon") // 2
    taps, rows, width = master.shape
    part = partial.reshape(taps, n_lat, n_q, 2, rows, width)
    max_norm = math.sqrt(float(partial.size))
    shard = jax.ShapeDtypeStruct(master.shape, jnp.float32)
    hops = n_q // 2
    half_type = jnp.bfloat16
    block = (n_lat, taps, rows, width)
    peers = n_q + n_lat - 1
    vmem = pl.BlockSpec(memory_space=pltpu.VMEM)
    copies = 64 + 8 * (n_q + n_lat)
    return pl.pallas_call(
        functools.partial(reduce_update_gather, n_lat, n_q, max_norm),
        out_shape=(
            jax.ShapeDtypeStruct((2, n_q) + block, half_type), shard, shard, shard, shard,
        ),
        in_specs=[vmem] * 4,
        out_specs=(vmem,) * 5,
        scratch_shapes=[
            pltpu.VMEM((taps, n_lat, n_q, rows, width), jnp.float32),
            pltpu.VMEM((n_q,) + block, half_type),
            pltpu.VMEM((hops,) + block, half_type),
            pltpu.VMEM((hops,) + block, half_type),
            pltpu.VMEM((n_lat - 1, taps, rows, width), half_type),
            pltpu.VMEM((n_lat - 1, taps, rows, width), half_type),
            pltpu.VMEM((3, 8, 128), jnp.float32),
            pltpu.VMEM((peers, 8, 128), jnp.float32),
            pltpu.SemaphoreType.DMA((copies,)),
            pltpu.SemaphoreType.DMA((copies,)),
        ],
        compiler_params=pltpu.CompilerParams(
            collective_id=0, has_side_effects=True, vmem_limit_bytes=60 * 1024 * 1024
        ),
        name="reduce_update_gather",
    )(part, master, one, two)


def per_device(activations, upstream, master, moment_one, moment_two):
    lat_rows = activations.shape[1]
    lon_cols = activations.shape[2]
    grad_flat = upstream.reshape(-1, upstream.shape[3])
    old_weights = master[:, ::-1].astype(jnp.bfloat16)
    old_full = lax.all_gather(old_weights, ("lat", "lon"), axis=0, tiled=True)
    act_wide, grad_wide = widened((activations, upstream))
    term_maker = input_taps(act_wide, grad_flat, lat_rows, lon_cols)
    partial = term_maker(jnp.int32(0), activations.shape[3])

    def by_tap(array):
        return jnp.transpose(array, (1, 0, 2))

    gathered, new_master, new_one, new_two, clipped = fused_update(
        by_tap(partial), by_tap(master), by_tap(moment_one), by_tap(moment_two)
    )
    new_weights = jnp.transpose(gathered, (2, 1, 0, 4, 3, 5)).reshape(
        activations.shape[3], gathered.shape[3], gathered.shape[5]
    )
    old_full, new_one = lax.optimization_barrier((old_full, new_one))
    input_grad = lax.conv_general_dilated(
        grad_wide,
        old_full.reshape(old_full.shape[0], 3, 3, old_full.shape[2]),
        (1, 1),
        "VALID",
        dimension_numbers=("NHWC", "OHWI", "NHWC"),
        preferred_element_type=jnp.float32,
    ).astype(jnp.bfloat16)
    return (
        input_grad, new_weights, by_tap(new_master), by_tap(new_one), by_tap(new_two),
        by_tap(clipped),
    )


def solution(mesh):
    in_specs = (
        P(None, "lat", "lon", None),
        P(None, "lat", "lon", None),
        P(("lat", "lon"), None, None),
        P(("lat", "lon"), None, None),
        P(("lat", "lon"), None, None),
    )
    out_specs = (
        P(None, "lat", "lon", None),
        P(),
        P(("lat", "lon"), None, None),
        P(("lat", "lon"), None, None),
        P(("lat", "lon"), None, None),
        P(("lat", "lon"), None, None),
    )
    return jax.shard_map(
        per_device, mesh=mesh, in_specs=in_specs, out_specs=out_specs, check_vma=False
    )
```

time: 432 us -> 241 us (0.56)
  waiting for transfers between devices: 282 us -> 0.02 us
  Pallas kernels: 0 us -> 166 us
  blocking collectives: 37.9 us -> 0 us
  local copies, waits for them, and re-layouts: 47.3 us -> 22.8 us
  starting transfers between devices: 14.5 us -> 0.04 us
    pallas_call x0 -> x2, Pallas kernels: none -> 166 us  [the longest x1 120 us: fused_update(): pl.pallas_call(functools.partial(reduce_update_gather, n_lat, n_q, max_no...]
    reduce_scatter x2 -> x0, waiting for transfers between devices: 135 us -> none  [the longest x1 95.2 us: per_device(): lax.psum_scatter(term_maker(jnp.int32(0), lax.axis_size('lat') * (shard_r...]
    all_gather x4 -> x1, waiting for transfers between devices: 123 us -> 0.01 us  [per_device(): old_full = lax.all_gather(old_weights, ('lat', 'lon'), axis=0, tiled=True)]
    psum x1 -> x0, blocking collectives: 37.9 us -> none  [per_device(): square_sum = lax.psum(jnp.sum(grad_shard * grad_shard), ('lat', 'lon'))]
    ppermute x8 -> x0, waiting for transfers between devices: 23.7 us -> none  [the longest x4 14.1 us: padded(): lax.ppermute(lax.slice_in_dim(block, 0, width, axis=dim), axis, backward)]
    reshape x9 -> x0, local copies, waits for them, and re-layouts: 18.5 us -> none  [pull_product(): windows.append(grad_wide[:, 2 - row_off:2 - row_off + lat_rows, 2 - col_o...]
    ppermute x8 -> x0, starting transfers between devices: 14.1 us -> none  [the longest x4 9.93 us: padded(): lax.ppermute(lax.slice_in_dim(block, 0, width, axis=dim), axis, backward)]
    slice x5 -> x0, local copies, waits for them, and re-layouts: 10.6 us -> none  [the longest x1 6.22 us: pull_product(): grad_wide[:, 2 - row_off:2 - row_off + lat_rows, 2 - col_off:2 - col_off...]
  transfers between devices with their start and end apart: 14 -> 1, of which waited for: 11 -> 0; matrix products, arithmetic and copies ran while one was open for 10% -> 17% of each run, Pallas kernels for 0% -> 69%
where the time goes in v1:
time: 241 us
  Pallas kernels  166 us (69%)
  matrix products  28.8 us (12%)
  local copies, waits for them, and re-layouts  22.8 us (9%)
  between operations  14.4 us (6%)
  other arithmetic  8.73 us (4%)
    pallas_call x1, Pallas kernels, fused_update(): pl.pallas_call(functools.partial(reduce_update_gather, n_lat, n_q, max_no...  120 us
    pallas_call x1, Pallas kernels, widened(): pl.pallas_call(functools.partial(halo_kernel, lax.axis_size('lat'), lax.a...  46 us
    dot_general x9, matrix products, input_compute(): lax.dot_general(tap_slab, grad_flat, (((0,), (0,)), ((), ())), preferred_...  18.3 us
    conv_general_dilated x1, matrix products, per_device(): lax.conv_general_dilated(grad_wide, old_full.reshape(old_full.shape[0], 3...  10.5 us
    unnamed x29, local copies, waits for them, and re-layouts  10.3 us
    transpose x1, local copies, waits for them, and re-layouts, per_device(): jnp.transpose(gathered, (2, 1, 0, 4, 3, 5))  5.32 us
  transfers between devices with their start and end apart: 1, of which 0 were waited for; matrix products, arithmetic and copies ran while one was open for 17% of the time, Pallas kernels for 69%

profile of v1, /device:TPU:0, one launch (start us, length us, event | category | flops | bytes accessed | tf_op | source)
XLA Modules:
  0.0 241.1 jit_solution(4245115340084497875)
XLA Ops:
  7.2 1.7 rev.5
  9.0 2.2 copy.118
  11.3 0.3 copy.54
  11.6 0.8 copy.119
  12.4 1.5 copy.65
  13.9 1.0 fusion.82
  14.8 0.2 copy.47.refs_0_
  15.4 46.0 %halo.1 = (bf16[2,4,90,512]{3,2,1,0:T(8,128)(2,1)S(1)}, bf16[2,4,90,512]{3,2,1,0:T(8,128)(2,1)S(1)}, bf16[2,4,4,512]{3,2,1,0:T(4,128)(2,1)S(1)}, bf16[2,4,4,512]...) custom-call(bf16[2,4,90,512]{3,2,1,0:T(8,128)(2,1)S(1)} %copy.47.ref, ...), custom_call_target="tpu_custom_call" | custom-call | tf_op jit(solution)/shard_map/halo/pallas_call | solution.py:57
  62.5 0.9 copy-done
  63.4 4.6 %fusion.5 = (bf16[6,4,92,512]{3,2,0,1:T(8,128)(2,1)S(1)}, bf16[4,6,92,512]{3,2,1,0:T(8,128)(2,1)S(1)}) fusion(bf16[4,1,92,512]{3,2,1,0:T(8,128)(2,1)S(1)} %maximum_bitcast_fusion.1, bf16[4,4,1,512]{3,2,1,0:T(2,128)(2,1)S(1)} %copy.55, bf16[4,4,90,512]{3,2,1,0:T(8,128)(2,1)S(1)} %copy.54, bf16[4,4,1,512]{3,2,1,0:T(2,128)(2,1)S(1)} %copy.53, ...), kind=kLoop, calls=%fused_computation.14 | loop fusion | flops 24870912 | bytes 9043974 | tf_op jit(solution)/shard_map/jit(_where)/select_n | solution.py:91
  67.9 1.7 copy.91
  69.7 0.9 pad.clone
  70.6 0.9 slice.144
  71.4 2.0 fusion.29
  73.5 2.0 fusion.35
  75.5 2.0 fusion.41
  77.5 2.0 fusion.47
  79.4 2.0 fusion.53
  81.5 2.0 fusion.59
  83.5 2.0 fusion.65
  85.5 2.1 fusion.71
  87.6 2.1 fusion.77
  89.7 120.2 %reduce_update_gather.1 = (bf16[2,4,4,9,16,512]{5,4,3,2,1,0:T(8,128)(2,1)}, f32[9,16,512]{2,1,0:T(8,128)}, f32[9,16,512]{2,1,0:T(8,128)}, f32[9,16,512]{2,1,0:T(8,128)}, f32[9,16,512]{2,1,0:T(8,128)}) custom-call(f32[9,4,4,2,16,512]{5,4,3,2,1,0:T(8,128)} %bitcast.61.part, f32[9,16,512]{2,1,0:T(8,128)} %bitcast.168, f32[9,16,512]{2,1,0:T(8,128)} %bitcast.169, ...), custom_call_target="tpu_custom_call" | custom-call | tf_op jit(solution)/shard_map/reduce_update_gather/pallas_call | solution.py:328
  210.0 5.3 %copy.81 = bf16[4,4,2,16,9,512]{5,3,2,1,0,4:T(8,128)(2,1)} copy(bf16[4,4,2,16,9,512]{5,3,4,0,1,2:T(8,128)(2,1)} %bitcast.167) | data formatting | bytes 9437184 | tf_op jit(solution)/shard_map/transpose | solution.py:370
  215.3 2.7 %fusion.1 = bf16[6,4,8,14,512]{4,1,3,2,0:T(4,128)(2,1)} fusion(bf16[6,4,7,2,512]{4,1,3,2,0:T(4,128)(2,1)S(1)} %copy-done.4, bf16[6,4,8,12,512]{4,1,3,2,0:T(4,128)(2,1)S(1)} %bitcast.164), kind=kLoop, calls=%fused_computation.9 | loop fusion | flops 8257536 | bytes 5455872 | tf_op jit(solution)/shard_map/conv_general_dilated | solution.py:374
  218.0 10.5 %select_convert_fusion = bf16[4,32,12,512]{3,1,2,0:T(8,128)(2,1)S(1)} fusion(pred[32,12]{0,1:T(8,128)(4,1)S(1)} %copy-done.9, bf16[512,3,3,512]{3,0,2,1:T(8,128)(2,1)} %bitcast.175, bf16[6,4,8,14,512]{4,1,3,2,0:T(4,128)(2,1)} %fusion.1), kind=kOutput, calls=%fused_computation.2 | convolution fusion | flops 7249330176 | bytes 9044352 | tf_op jit(solution)/shard_map/conv_general_dilated | solution.py:374
  228.5 1.2 copy.80
  229.8 1.6 slice_bitcast_fusion
  231.4 0.7 copy.132
  232.1 0.7 copy.133
  232.8 0.7 copy.134
  233.6 0.7 copy.135
  (52 shorter events, 1.3 us)
Async XLA Ops:
  7.2 4.1 %copy-start.2 = (bf16[4,4,90,512]{3,1,2,0:T(4,128)(2,1)S(1)}, bf16[4,4,90,512]{3,1,2,0:T(4,128)(2,1)}, u32[]{:S(2)}) copy-start(bf16[4,4,90,512]{3,1,2,0:T(4,128)(2,1)} %param.6) | copy-start | bytes 4423684
  7.2 210.8 %all-gather.2.cloned.1.call-start = ((), (), s32[]{:S(2)}) async-start(), calls=%async_computation | async-start | bytes 4866048 | tf_op jit(solution)/shard_map/all_gather | solution.py:359
  9.0 2.6 %copy-start.1 = (bf16[4,4,90,512]{3,1,2,0:T(4,128)(2,1)S(1)}, bf16[4,4,90,512]{3,1,2,0:T(4,128)(2,1)}, u32[]{:S(2)}) copy-start(bf16[4,4,90,512]{3,1,2,0:T(4,128)(2,1)} %param.5) | copy-start | bytes 4423684
  61.9 1.4 copy-start
  69.7 1.8 copy-start.3
  209.9 5.3 %copy-start.4 = (bf16[6,4,7,2,512]{4,1,3,2,0:T(4,128)(2,1)S(1)}, bf16[6,4,7,2,512]{4,1,3,2,0:T(4,128)(2,1)}, u32[]{:S(2)}) copy-start(bf16[6,4,7,2,512]{4,1,3,2,0:T(4,128)(2,1)} %slice.144) | copy-start | bytes 1032196
  215.3 2.7 %copy-start.9 = (pred[32,12]{0,1:T(8,128)(4,1)S(1)}, pred[32,12]{0,1:T(8,128)(4,1)}, u32[]{:S(2)}) copy-start(pred[32,12]{0,1:T(8,128)(4,1)} %constant.23) | copy-start | bytes 1156
  228.5 2.9 %copy-start.8 = (f32[9,16,512]{2,1,0:T(8,128)S(1)}, f32[9,16,512]{2,1,0:T(8,128)}, u32[]{:S(2)}) copy-start(f32[9,16,512]{2,1,0:T(8,128)} %get-tuple-element.32) | copy-start | bytes 884740
  229.8 2.4 copy-start.7
  229.8 3.1 %copy-start.6 = (f32[9,16,512]{2,1,0:T(8,128)S(1)}, f32[9,16,512]{2,1,0:T(8,128)}, u32[]{:S(2)}) copy-start(f32[9,16,512]{2,1,0:T(8,128)} %get-tuple-element.34) | copy-start | bytes 884740
  229.8 3.8 %copy-start.5 = (f32[9,16,512]{2,1,0:T(8,128)S(1)}, f32[9,16,512]{2,1,0:T(8,128)}, u32[]{:S(2)}) copy-start(f32[9,16,512]{2,1,0:T(8,128)} %get-tuple-element.35) | copy-start | bytes 884740
Sparse Core Ops, SparseCore 0:
  11.6 70.1 all-gather.1
